TPU v7x, 128 devices: a whole 4x4x4 slice. The times are simulated.
128 devices in a mesh: fsdp: 16 (over z, x_lo, core), cols: 8 (over y, x_hi).
Axes of the slice: x: 4 (x_hi: 2, x_lo: 2; x = x_hi * 2 + x_lo), y: 4, z: 4, core: 2. Of those that a mesh axis runs over, the one named last changes fastest.
Arguments:
- weight_query: bfloat16 [5120, 5120], P('fsdp', 'cols'), may hold values from -0.078125 to 0.078125
- low_query: bfloat16 [5120, 32], P('fsdp'), may hold values from -0.078125 to 0.078125
- high_query: bfloat16 [32, 5120], P(None, 'cols'), may hold values from -1 to 1
- weight_key: bfloat16 [5120, 5120], P('fsdp', 'cols'), may hold values from -0.078125 to 0.078125
- low_key: bfloat16 [5120, 32], P('fsdp'), may hold values from -0.078125 to 0.078125
- high_key: bfloat16 [32, 5120], P(None, 'cols'), may hold values from -1 to 1
- weight_value: bfloat16 [5120, 5120], P('fsdp', 'cols'), may hold values from -0.078125 to 0.078125
- low_value: bfloat16 [5120, 32], P('fsdp'), may hold values from -0.078125 to 0.078125
- high_value: bfloat16 [32, 5120], P(None, 'cols'), may hold values from -1 to 1
- weight_mixed: bfloat16 [5120, 5120], P('cols', 'fsdp'), may hold values from -0.078125 to 0.078125
- low_mixed: bfloat16 [5120, 32], P('cols'), may hold values from -0.078125 to 0.078125
- high_mixed: bfloat16 [32, 5120], P(None, 'fsdp'), may hold values from -1 to 1
- norm_train: float32 [5120], P(('fsdp', 'cols')), may hold values from 0.25 to 1.75
- norm_step: float32 [5120], P(('fsdp', 'cols')), may hold values from -0.3 to 0.3
Outputs:
- ready_query: bfloat16 [5120, 5120], P(None, 'cols')
- ready_key: bfloat16 [5120, 5120], P(None, 'cols')
- ready_value: bfloat16 [5120, 5120], P(None, 'cols')
- ready_mixed: bfloat16 [5120, 5120], P('cols')
- serve_norm: bfloat16 [5120], replicated
All inputs are finite; a program needn't handle non-finite values.
Results may differ from a plain program's by a relative error of at most 0.001.
Values may be sent and summed in bfloat16 or wider, within the bound.
No kernel may reach another device: no remote copies, remote signals or barrier semaphores. Data moves between devices by JAX's collectives and lax.ppermute only.
A program may use at most 192 MiB of HBM per device.

v0:
```python
import jax
import jax.numpy as jnp
from jax import lax
from jax.experimental import pallas as pl
from jax.experimental.pallas import tpu as pltpu
from jax.sharding import PartitionSpec as P


mix_rate = 2.0
BLOCK = 320
WIDTH = 640
HEAD = 256
B_ROWS = BLOCK + HEAD
A_ROWS = 3 * BLOCK - HEAD

Z_UP = [(f, (f + 4) % 16) for f in range(16)]
Z_DOWN = [(f, (f - 4) % 16) for f in range(16)]
X_SWAP = [(f, f ^ 2) for f in range(16)]
CORE_SWAP = [(f, f ^ 1) for f in range(16)]
HI_SWAP = [(k, k ^ 1) for k in range(8)]


def y_up(s):
    return [(k, (k + 2 * s) % 8) for k in range(8)]


def send(a, perm, axis="fsdp"):
    return lax.ppermute(a, axis, perm)


def updated(weight, low, high):
    product = jnp.dot(low, high, preferred_element_type=jnp.float32)
    return (weight.astype(jnp.float32) + mix_rate * product).astype(jnp.bfloat16)


PARTS = {
    "b": ((0, BLOCK, 0, 0), (BLOCK, B_ROWS, 1, 0)),
    "a": ((0, BLOCK, 2, 0), (BLOCK, 2 * BLOCK, 3, 0), (2 * BLOCK, A_ROWS, 1, HEAD)),
}


def rows_of(piece):
    return piece[2] - piece[1]


def copies_of(piece, ref, base, outs, dc, place):
    kind, low, high, dz, dx = piece
    z, x, c = place
    chip = lax.rem(z - dz + 4, 4) * 2 + (x + dx - 2 * x * dx)
    core = c + dc - 2 * c * dc
    found = []
    for first, end, which, row in PARTS[kind]:
        lo, hi = max(first, low), min(end, high)
        if lo >= hi:
            continue
        n, row = hi - lo, row + lo - first
        source = ref.at[pl.ds(base + lo - low, n), :]
        if which == 3:
            at = (pl.ds(pl.multiple_of(core * BLOCK + row, 16), n), pl.ds(pl.multiple_of(chip * WIDTH, 128), WIDTH))
        else:
            at = (pl.ds(pl.multiple_of(chip * (2 * BLOCK) + core * BLOCK + row, 16), n), slice(None))
        found.append((source, outs[which].at[at]))
    return found


def assemble(place, own, other, outs, stack=True):
    n_own, n_other = len(own), len(other)
    rows = sum(rows_of(p) for p, _ in own)
    before = [] if outs is None else list(outs)

    def body(place_ref, *refs):
        own_refs, other_refs = refs[:n_own], refs[n_own : n_own + n_other]
        refs = refs[n_own + n_other + len(before) :]
        out_refs, refs = refs[:4], refs[4:]
        stack_ref, load_sem, store_sem = refs if own else (None, None, refs[0])
        where = (place_ref[0], place_ref[1], place_ref[2])
        loads, base = [], 0
        for i, ((piece, _), ref) in enumerate(zip(own, own_refs)):
            n = rows_of(piece)
            loads.append(pltpu.make_async_copy(ref, stack_ref.at[pl.ds(base, n), :], load_sem.at[i]))
            loads[-1].start()
            base += n
        stores = []

        def put(piece, ref, base, dc):
            for source, target in copies_of(piece, ref, base, out_refs, dc, where):
                stores.append(pltpu.make_async_copy(source, target, store_sem.at[len(stores)]))
                stores[-1].start()

        for (pieces, _), ref in zip(other, other_refs):
            base = 0
            for piece in pieces:
                put(piece, ref, base, 1)
                base += rows_of(piece)
        base = 0
        for load, (piece, _) in zip(loads, own):
            load.wait()
            put(piece, stack_ref, base, 0)
            base += rows_of(piece)
        for store in stores:
            store.wait()

    shapes = [jax.ShapeDtypeStruct((16 * BLOCK, WIDTH), jnp.bfloat16)] * 3
    shapes.append(jax.ShapeDtypeStruct((WIDTH, 16 * BLOCK), jnp.bfloat16))
    any_spec = pl.BlockSpec(memory_space=pl.ANY)
    vmem_spec = pl.BlockSpec(memory_space=pltpu.VMEM)
    out_specs = [any_spec] * 4
    scratch = []
    if own and stack:
        shapes.append(jax.ShapeDtypeStruct((rows, WIDTH), jnp.bfloat16))
        out_specs.append(vmem_spec)
    elif own:
        scratch.append(pltpu.VMEM((rows, WIDTH), jnp.bfloat16))
    if own:
        scratch.append(pltpu.SemaphoreType.DMA((n_own,)))
    pieces = [p for p, _ in own] + [p for many, _ in other for p in many]
    scratch.append(pltpu.SemaphoreType.DMA((3 * len(pieces),)))
    call = pl.pallas_call(
        body,
        out_shape=shapes,
        in_specs=[pl.BlockSpec(memory_space=pltpu.SMEM)] + [any_spec] * n_own + [vmem_spec] * n_other + [any_spec] * len(before),
        out_specs=out_specs,
        scratch_shapes=scratch,
        input_output_aliases={1 + n_own + n_other + i: i for i in range(len(before))},
        compiler_params=pltpu.CompilerParams(vmem_limit_bytes=12 << 20),
    )
    result = call(place, *[v for _, v in own], *[v for _, v in other], *before)
    return result[:4], (result[4] if own and stack else None)


def gathered_norm(norm_train, norm_step, z, x, c):
    mine = (norm_train + norm_step).astype(jnp.bfloat16)
    rows = jnp.pad(mine, (0, 88))[None, :]
    rows = jnp.concatenate([rows] + [send(rows, y_up(s), "cols") for s in (1, 2, 3)], 0)
    rows = jnp.concatenate([rows, send(rows, HI_SWAP, "cols")], 0)
    rows = jnp.concatenate([rows, send(rows, CORE_SWAP)], 0)
    rows = jnp.concatenate([rows, send(rows, X_SWAP)], 0)
    below = send(rows, Z_UP)
    rows = jnp.concatenate([rows, below, send(below, Z_UP), send(rows, Z_DOWN)], 0)
    k = lax.axis_index("cols")
    y, hi = k // 2, k % 2
    r = lax.iota(jnp.int32, 128)
    col = ((y - r % 4) % 4) * 2 + (hi ^ (r // 4 % 2))
    part = ((z - r // 32) % 4) * 4 + (x ^ (r // 16 % 2)) * 2 + (c ^ (r // 8 % 2))
    place = (lax.iota(jnp.int32, 128)[:, None] == (part * 8 + col)[None, :]).astype(jnp.bfloat16)
    ordered = jnp.dot(place, rows, preferred_element_type=jnp.float32).astype(jnp.bfloat16)
    return ordered[:, :40].reshape(5120)


def per_device(
    weight_query, low_query, high_query,
    weight_key, low_key, high_key,
    weight_value, low_value, high_value,
    weight_mixed, low_mixed, high_mixed,
    norm_train, norm_step,
):
    f = lax.axis_index("fsdp")
    z, x, c = f // 4, f // 2 % 2, f % 2
    place = jnp.stack([z, x, c]).astype(jnp.int32)

    b = jnp.concatenate(
        [
            updated(weight_query, low_query, high_query),
            updated(weight_key[:HEAD], low_key[:HEAD], high_key),
        ],
        0,
    )
    mixed = updated(weight_mixed, low_mixed, high_mixed)
    keep = lax.dynamic_slice(mixed, (c * BLOCK, 0), (BLOCK, BLOCK))
    give = lax.dynamic_slice(mixed, ((1 - c) * BLOCK, 0), (BLOCK, BLOCK))
    got = send(give, CORE_SWAP)
    left = jnp.where(c == 0, keep, got)
    right = jnp.where(c == 0, got, keep)
    a = jnp.concatenate(
        [
            updated(weight_value, low_value, high_value),
            jnp.concatenate([left, right], 1),
            updated(weight_key[HEAD:], low_key[HEAD:], high_key),
        ],
        0,
    )

    hb, ha = B_ROWS // 2, A_ROWS // 2
    b_up, b_down, b_x = send(b, Z_UP), send(b, Z_DOWN), send(b, X_SWAP)
    a_up, a_down, a_x = send(a, Z_UP), send(a, Z_DOWN), send(a, X_SWAP)
    b_up2, b_down2 = send(b_up[:hb], Z_UP), send(b_down[hb:], Z_DOWN)
    bx_up, bx_down = send(b_up, X_SWAP), send(b_down, X_SWAP)
    ax_up, ax_down = send(a_x, Z_UP), send(a_x, Z_DOWN)
    a_up2, a_down2 = send(a_up[:ha], Z_UP), send(a_down[ha:], Z_DOWN)
    bx_up2, bx_down2 = send(b_up2, X_SWAP), send(b_down2, X_SWAP)
    ax_up2, ax_down2 = send(ax_up[:ha], Z_UP), send(ax_down[ha:], Z_DOWN)

    serve_norm = gathered_norm(norm_train, norm_step, z, x, c)

    def whole(kind, dz, dx, v):
        return ((kind, 0, B_ROWS if kind == "b" else A_ROWS, dz, dx), v)

    def top(kind, dx, v):
        return ((kind, 0, hb if kind == "b" else ha, 2, dx), v)

    def bottom(kind, dx, v):
        return ((kind, hb, B_ROWS, 2, dx) if kind == "b" else (kind, ha, A_ROWS, 2, dx), v)

    def swapped(own, stack):
        return ([p for p, _ in own], send(stack, CORE_SWAP))

    own1 = [whole("b", 0, 0, b), whole("a", 0, 0, a), whole("b", 1, 0, b_up), whole("b", 3, 0, b_down), whole("b", 0, 1, b_x)]
    outs, stack1 = assemble(place, own1, [], None)
    own2 = [whole("a", 1, 0, a_up), whole("a", 3, 0, a_down), whole("a", 0, 1, a_x), top("b", 0, b_up2), bottom("b", 0, b_down2)]
    outs, stack2 = assemble(place, own2, [swapped(own1, stack1)], outs)
    own3 = [whole("a", 1, 1, ax_up), whole("a", 3, 1, ax_down), whole("b", 1, 1, bx_up), whole("b", 3, 1, bx_down), top("a", 0, a_up2), bottom("a", 0, a_down2)]
    outs, stack3 = assemble(place, own3, [swapped(own2, stack2)], outs)
    own4 = [top("a", 1, ax_up2), bottom("a", 1, ax_down2), top("b", 1, bx_up2), bottom("b", 1, bx_down2)]
    late = [([p], send(v, CORE_SWAP)) for p, v in own4]
    outs, _ = assemble(place, own4, [swapped(own3, stack3)], outs, stack=False)
    outs, _ = assemble(place, [], late, outs)
    return (*outs, serve_norm)


def solution(mesh):
    in_specs = (
        P("fsdp", "cols"), P("fsdp", None), P(None, "cols"),
        P("fsdp", "cols"), P("fsdp", None), P(None, "cols"),
        P("fsdp", "cols"), P("fsdp", None), P(None, "cols"),
        P("cols", "fsdp"), P("cols", None), P(None, "fsdp"),
        P(("fsdp", "cols")), P(("fsdp", "cols")),
    )
    out_specs = (P(None, "cols"), P(None, "cols"), P(None, "cols"), P("cols", None), P())

    return jax.shard_map(per_device, mesh=mesh, in_specs=in_specs, out_specs=out_specs, check_vma=False)
```

profile of v0, /device:TPU:1, one launch (start us, length us, event | category | flops | bytes accessed | tf_op | source)
XLA Modules:
  0.0 177.9 jit_solution(17017722894178206059)
XLA Ops:
  4.1 4.6 %collective-permute-start.12 = (bf16[576,640]{1,0:T(8,128)(2,1)S(1)}, bf16[576,640]{1,0:T(8,128)(2,1)S(1)}, u32[]{:S(2)}, u32[]{:S(2)}) collective-permute-start(bf16[576,640]{1,0:T(8,128)(2,1)S(1)} %pad_maximum_fusion.1.refs_0_), channel_id=1, source_target_pairs={{0,96},{8,104},{16,112},{24,120},{32,0},{40,8},{48,16},{56,24},{64... | collective-permute-start | bytes 2211848 | tf_op jit(solution)/shard_map/ppermute | solution.py:28
  10.0 2.1 %copy.41 = f32[640,320]{1,0:T(8,128)} copy(bf16[640,320]{0,1:T(8,128)(2,1)} %param.23) | data formatting | bytes 1228800 | tf_op jit(solution)/shard_map/convert_element_type | solution.py:33
  12.1 1.6 fusion.3
  15.7 2.1 %fusion.5 = bf16[320,640]{1,0:T(8,128)(2,1)} fusion(bf16[320,32]{0,1:T(8,128)(2,1)S(1)} %copy-done.4, bf16[32,640]{1,0:T(8,128)(2,1)S(1)} %copy-done.2, bf16[320,640]{1,0:T(8,128)(2,1)} %param.20), kind=kOutput, calls=%fused_computation.9 | convolution fusion | flops 13926400 | bytes 880640 | tf_op jit(solution)/shard_map/dot_general | solution.py:32
  21.1 2.8 %collective-permute-done.12.refs_3_ = bf16[576,640]{1,0:T(8,128)(2,1)S(1)} collective-permute-done((bf16[576,640]{1,0:T(8,128)(2,1)S(1)}, bf16[576,640]{1,0:T(8,128)(2,1)S(1)}, u32[]{:S(2)}, u32[]{:S(2)}) %collective-permute-start.12) | collective-permute-done | bytes 737312 | tf_op jit(solution)/shard_map/ppermute | solution.py:28
  24.0 3.1 %collective-permute-done.8.refs_2_ = bf16[576,640]{1,0:T(8,128)(2,1)S(1)} collective-permute-done((bf16[576,640]{1,0:T(8,128)(2,1)S(1)}, bf16[576,640]{1,0:T(8,128)(2,1)S(1)}, u32[]{:S(2)}, u32[]{:S(2)}) %collective-permute-start.8) | collective-permute-done | bytes 737312 | tf_op jit(solution)/shard_map/ppermute | solution.py:28
  27.1 4.1 %shard_map.173 = (bf16[5120,640]{1,0:T(8,128)(2,1)}, bf16[5120,640]{1,0:T(8,128)(2,1)}, bf16[5120,640]{1,0:T(8,128)(2,1)}, bf16[640,5120]{1,0:T(8,128)(2,1)}, bf16[3008,640]{1,0:T(8,128)(2,1)S(1)}) custom-call(s32[3]{0:T(128)S(1)} %pad_add_fusion.place_ref, bf16[576,640]{1,0:T(8,128)(2,1)S(1)} %pad_maximum_fusion.1.refs_0_, ...), custom_call_target="tpu_custom_call" | custom-call | tf_op jit(solution)/shard_map/pallas_call | solution.py:127
  31.1 1.9 %collective-permute-start.23 = (bf16[3008,640]{1,0:T(8,128)(2,1)S(1)}, bf16[3008,640]{1,0:T(8,128)(2,1)S(1)}, u32[]{:S(2)}, u32[]{:S(2)}) collective-permute-start(bf16[3008,640]{1,0:T(8,128)(2,1)S(1)} %get-tuple-element.28), channel_id=1, source_target_pairs={{0,8},{8,0},{16,24},{24,16},{32,40},{40,32},{48,56},{56,48},{64,72... | collective-permute-start | bytes 11550728 | tf_op jit(solution)/shard_map/ppermute | solution.py:28
  34.2 2.7 %collective-permute-start.20 = (bf16[704,640]{1,0:T(8,128)(2,1)S(1)}, bf16[704,640]{1,0:T(8,128)(2,1)S(1)}, u32[]{:S(2)}, u32[]{:S(2)}) collective-permute-start(bf16[704,640]{1,0:T(8,128)(2,1)S(1)} %pad_maximum_fusion.refs_1_), channel_id=1, source_target_pairs={{0,96},{8,104},{16,112},{24,120},{32,0},{40,8},{48,16},{56,24},{64... | collective-permute-start | bytes 2703368 | tf_op jit(solution)/shard_map/ppermute | solution.py:28
  37.3 17.2 %collective-permute-done.1.refs_2_ = bf16[704,640]{1,0:T(8,128)(2,1)S(1)} collective-permute-done((bf16[704,640]{1,0:T(8,128)(2,1)S(1)}, bf16[704,640]{1,0:T(8,128)(2,1)S(1)}, u32[]{:S(2)}, u32[]{:S(2)}) %collective-permute-start.1) | collective-permute-done | bytes 901152 | tf_op jit(solution)/shard_map/ppermute | solution.py:28
  54.5 2.1 %collective-permute-done.18.refs_0_ = bf16[704,640]{1,0:T(8,128)(2,1)S(1)} collective-permute-done((bf16[704,640]{1,0:T(8,128)(2,1)S(1)}, bf16[704,640]{1,0:T(8,128)(2,1)S(1)}, u32[]{:S(2)}, u32[]{:S(2)}) %collective-permute-start.18) | collective-permute-done | bytes 901152 | tf_op jit(solution)/shard_map/ppermute | solution.py:28
  56.6 6.9 %collective-permute-done.13.refs_4_ = bf16[288,640]{1,0:T(8,128)(2,1)S(1)} collective-permute-done((bf16[288,640]{1,0:T(8,128)(2,1)S(1)}, bf16[288,640]{1,0:T(8,128)(2,1)S(1)}, u32[]{:S(2)}, u32[]{:S(2)}) %collective-permute-start.13) | collective-permute-done | bytes 368672 | tf_op jit(solution)/shard_map/ppermute | solution.py:28
  64.9 4.7 %shard_map.174 = (bf16[5120,640]{1,0:T(8,128)(2,1)}, bf16[5120,640]{1,0:T(8,128)(2,1)}, bf16[5120,640]{1,0:T(8,128)(2,1)}, bf16[640,5120]{1,0:T(8,128)(2,1)}, bf16[2688,640]{1,0:T(8,128)(2,1)S(1)}) custom-call(s32[3]{0:T(128)S(1)} %pad_add_fusion.place_ref, ...), custom_call_target="tpu_custom_call", output_to_operand_aliasing={{0}: (7, {}), {1}: (8, {}), {2}: (9, {}), {3}: (10, {})} | custom-call | tf_op jit(solution)/shard_map/pallas_call | solution.py:127
  69.6 1.9 %collective-permute-start.24 = (bf16[2688,640]{1,0:T(8,128)(2,1)S(1)}, bf16[2688,640]{1,0:T(8,128)(2,1)S(1)}, u32[]{:S(2)}, u32[]{:S(2)}) collective-permute-start(bf16[2688,640]{1,0:T(8,128)(2,1)S(1)} %get-tuple-element.33), channel_id=1, source_target_pairs={{0,8},{8,0},{16,24},{24,16},{32,40},{40,32},{48,56},{56,48},{64,72... | collective-permute-start | bytes 10321928 | tf_op jit(solution)/shard_map/ppermute | solution.py:28
  73.0 2.7 %collective-permute-start.5 = (bf16[704,640]{1,0:T(8,128)(2,1)S(1)}, bf16[704,640]{1,0:T(8,128)(2,1)S(1)}, u32[]{:S(2)}, u32[]{:S(2)}) collective-permute-start(bf16[704,640]{1,0:T(8,128)(2,1)S(1)} %collective-permute-done.1.refs_2_), channel_id=1, source_target_pairs={{0,96},{8,104},{16,112},{24,120},{32,0},{40,8},{48,16},{56,24},{64... | collective-permute-start | bytes 2703368 | tf_op jit(solution)/shard_map/ppermute | solution.py:28
  75.7 13.7 %collective-permute-done.16.refs_2_ = bf16[576,640]{1,0:T(8,128)(2,1)S(1)} collective-permute-done((bf16[576,640]{1,0:T(8,128)(2,1)S(1)}, bf16[576,640]{1,0:T(8,128)(2,1)S(1)}, u32[]{:S(2)}, u32[]{:S(2)}) %collective-permute-start.16) | collective-permute-done | bytes 737312 | tf_op jit(solution)/shard_map/ppermute | solution.py:28
  89.5 15.8 %collective-permute-done.17.refs_3_ = bf16[576,640]{1,0:T(8,128)(2,1)S(1)} collective-permute-done((bf16[576,640]{1,0:T(8,128)(2,1)S(1)}, bf16[576,640]{1,0:T(8,128)(2,1)S(1)}, u32[]{:S(2)}, u32[]{:S(2)}) %collective-permute-start.17) | collective-permute-done | bytes 737312 | tf_op jit(solution)/shard_map/ppermute | solution.py:28
  105.3 1.7 collective-permute-start.21
  107.0 9.2 %collective-permute-done.21.refs_5_ = bf16[352,640]{1,0:T(8,128)(2,1)S(1)} collective-permute-done((bf16[352,640]{1,0:T(8,128)(2,1)S(1)}, bf16[352,640]{1,0:T(8,128)(2,1)S(1)}, u32[]{:S(2)}, u32[]{:S(2)}) %collective-permute-start.21) | collective-permute-done | bytes 450592 | tf_op jit(solution)/shard_map/ppermute | solution.py:28
  116.3 7.4 %shard_map.175 = (bf16[5120,640]{1,0:T(8,128)(2,1)}, bf16[5120,640]{1,0:T(8,128)(2,1)}, bf16[5120,640]{1,0:T(8,128)(2,1)}, bf16[640,5120]{1,0:T(8,128)(2,1)}, bf16[3264,640]{1,0:T(8,128)(2,1)}) custom-call(s32[3]{0:T(128)S(1)} %pad_add_fusion.place_ref, ...), custom_call_target="tpu_custom_call", output_to_operand_aliasing={{0}: (8, {}), {1}: (9, {}), {2}: (10, {}), {3}: (11, {})} | custom-call | tf_op jit(solution)/shard_map/pallas_call | solution.py:127
  123.7 1.9 %collective-permute-start.25 = (bf16[3264,640]{1,0:T(8,128)(2,1)}, bf16[3264,640]{1,0:T(8,128)(2,1)}, u32[]{:S(2)}, u32[]{:S(2)}) collective-permute-start(bf16[3264,640]{1,0:T(8,128)(2,1)} %get-tuple-element.38), channel_id=1, source_target_pairs={{0,8},{8,0},{16,24},{24,16},{32,40},{40,32},{48,56},{56,48},{64,72... | collective-permute-start | bytes 12533768 | tf_op jit(solution)/shard_map/ppermute | solution.py:28
  125.8 3.0 %collective-permute-start.6 = (bf16[352,640]{1,0:T(8,128)(2,1)S(1)}, bf16[352,640]{1,0:T(8,128)(2,1)S(1)}, u32[]{:S(2)}, u32[]{:S(2)}) collective-permute-start(bf16[352,640]{1,0:T(8,128)(2,1)S(1)} %slice.45), channel_id=1, source_target_pairs={{0,96},{8,104},{16,112},{24,120},{32,0},{40,8},{48,16},{56,24},{64... | collective-permute-start | bytes 1351688 | tf_op jit(solution)/shard_map/ppermute | solution.py:28
  130.1 2.6 %collective-permute-start.27 = (bf16[1,128]{1,0:T(2,128)(2,1)S(1)}, bf16[1,128]{1,0:T(2,128)(2,1)S(1)}, u32[]{:S(2)}, u32[]{:S(2)}) collective-permute-start(bf16[1,128]{1,0:T(2,128)(2,1)S(1)} %pad_bitcast_fusion), channel_id=1, source_target_pairs={{0,4},{1,5},{2,6},{3,7},{4,0},{5,1},{6,2},{7,3},{8,12},{9,13},{10,... | collective-permute-start | bytes 776 | tf_op jit(solution)/shard_map/ppermute | solution.py:28
  135.5 2.5 %collective-permute-start.29 = (bf16[4,128]{1,0:T(4,128)(2,1)S(1)}, bf16[4,128]{1,0:T(4,128)(2,1)S(1)}, u32[]{:S(2)}, u32[]{:S(2)}) collective-permute-start(bf16[4,128]{1,0:T(4,128)(2,1)S(1)} %pad_maximum_fusion.2), channel_id=1, source_target_pairs={{0,1},{1,0},{2,3},{3,2},{4,5},{5,4},{6,7},{7,6},{8,9},{9,8},{10,11... | collective-permute-start | bytes 3080 | tf_op jit(solution)/shard_map/ppermute | solution.py:28
  139.5 3.2 %collective-permute-start.30 = (bf16[8,128]{1,0:T(8,128)(2,1)S(1)}, bf16[8,128]{1,0:T(8,128)(2,1)S(1)}, u32[]{:S(2)}, u32[]{:S(2)}) collective-permute-start(bf16[8,128]{1,0:T(8,128)(2,1)S(1)} %concatenate.32), channel_id=1, source_target_pairs={{0,8},{8,0},{16,24},{24,16},{32,40},{40,32},{48,56},{56,48},{64,72... | collective-permute-start | bytes 6152 | tf_op jit(solution)/shard_map/ppermute | solution.py:28
  146.2 2.7 %collective-permute-start.34 = (bf16[32,128]{1,0:T(8,128)(2,1)S(1)}, bf16[32,128]{1,0:T(8,128)(2,1)S(1)}, u32[]{:S(2)}, u32[]{:S(2)}) collective-permute-start(bf16[32,128]{1,0:T(8,128)(2,1)S(1)} %concatenate.34), channel_id=1, source_target_pairs={{0,96},{8,104},{16,112},{24,120},{32,0},{40,8},{48,16},{56,24},{64... | collective-permute-start | bytes 24584 | tf_op jit(solution)/shard_map/ppermute | solution.py:28
  151.1 2.5 %collective-permute-done.33 = bf16[32,128]{1,0:T(8,128)(2,1)S(1)} collective-permute-done((bf16[32,128]{1,0:T(8,128)(2,1)S(1)}, bf16[32,128]{1,0:T(8,128)(2,1)S(1)}, u32[]{:S(2)}, u32[]{:S(2)}) %collective-permute-start.33) | collective-permute-done | bytes 8224 | tf_op jit(solution)/shard_map/ppermute | solution.py:28
  154.8 4.1 %collective-permute-start.4 = (bf16[352,640]{1,0:T(8,128)(2,1)S(1)}, bf16[352,640]{1,0:T(8,128)(2,1)S(1)}, u32[]{:S(2)}, u32[]{:S(2)}) collective-permute-start(bf16[352,640]{1,0:T(8,128)(2,1)S(1)} %collective-permute-done.3.refs_0_), channel_id=1, source_target_pairs={{0,8},{8,0},{16,24},{24,16},{32,40},{40,32},{48,56},{56,48},{64,72... | collective-permute-start | bytes 1351688 | tf_op jit(solution)/shard_map/ppermute | solution.py:28
  159.0 5.0 %collective-permute-start.11 = (bf16[288,640]{1,0:T(8,128)(2,1)S(1)}, bf16[288,640]{1,0:T(8,128)(2,1)S(1)}, u32[]{:S(2)}, u32[]{:S(2)}) collective-permute-start(bf16[288,640]{1,0:T(8,128)(2,1)S(1)} %collective-permute-done.10.refs_2_), channel_id=1, source_target_pairs={{0,8},{8,0},{16,24},{24,16},{32,40},{40,32},{48,56},{56,48},{64,72... | collective-permute-start | bytes 1105928 | tf_op jit(solution)/shard_map/ppermute | solution.py:28
  165.3 3.5 %collective-permute-start.15 = (bf16[288,640]{1,0:T(8,128)(2,1)S(1)}, bf16[288,640]{1,0:T(8,128)(2,1)S(1)}, u32[]{:S(2)}, u32[]{:S(2)}) collective-permute-start(bf16[288,640]{1,0:T(8,128)(2,1)S(1)} %collective-permute-done.14.refs_3_), channel_id=1, source_target_pairs={{0,8},{8,0},{16,24},{24,16},{32,40},{40,32},{48,56},{56,48},{64,72... | collective-permute-start | bytes 1105928 | tf_op jit(solution)/shard_map/ppermute | solution.py:28
  170.0 5.8 %shard_map.176 = (bf16[5120,640]{1,0:T(8,128)(2,1)}, bf16[5120,640]{1,0:T(8,128)(2,1)}, bf16[5120,640]{1,0:T(8,128)(2,1)}, bf16[640,5120]{1,0:T(8,128)(2,1)}) custom-call(s32[3]{0:T(128)S(1)} %pad_add_fusion.place_ref, bf16[352,640]{1,0:T(8,128)(2,1)S(1)} %collective-permute-done.3.refs_0_, ...), custom_call_target="tpu_custom_call", output_to_operand_aliasing={{0}: (6, {}), {1}: (7, {}), {2}: (8, {}), {3}: (9, {})} | custom-call | tf_op jit(solution)/shard_map/pallas_call | solution.py:127
  175.9 1.8 %shard_map.177 = (bf16[5120,640]{1,0:T(8,128)(2,1)}, bf16[5120,640]{1,0:T(8,128)(2,1)}, bf16[5120,640]{1,0:T(8,128)(2,1)}, bf16[640,5120]{1,0:T(8,128)(2,1)}) custom-call(s32[3]{0:T(128)S(1)} %pad_add_fusion.place_ref, bf16[352,640]{1,0:T(8,128)(2,1)S(1)} %collective-permute-done.4.refs_0_, ...), custom_call_target="tpu_custom_call", output_to_operand_aliasing={{0}: (5, {}), {1}: (6, {}), {2}: (7, {}), {3}: (8, {})} | custom-call | tf_op jit(solution)/shard_map/pallas_call | solution.py:127
  (86 shorter events, 29.8 us)
Async XLA Ops:
  4.1 19.8 %collective-permute-start.12 = (bf16[576,640]{1,0:T(8,128)(2,1)S(1)}, bf16[576,640]{1,0:T(8,128)(2,1)S(1)}, u32[]{:S(2)}, u32[]{:S(2)}) collective-permute-start(bf16[576,640]{1,0:T(8,128)(2,1)S(1)} %pad_maximum_fusion.1.refs_0_), channel_id=1, source_target_pairs={{0,96},{8,104},{16,112},{24,120},{32,0},{40,8},{48,16},{56,24},{64... | collective-permute-start | bytes 2211848 | tf_op jit(solution)/shard_map/ppermute | solution.py:28
  8.8 18.3 %collective-permute-start.8 = (bf16[576,640]{1,0:T(8,128)(2,1)S(1)}, bf16[576,640]{1,0:T(8,128)(2,1)S(1)}, u32[]{:S(2)}, u32[]{:S(2)}) collective-permute-start(bf16[576,640]{1,0:T(8,128)(2,1)S(1)} %pad_maximum_fusion.1.refs_0_), channel_id=1, source_target_pairs={{0,32},{8,40},{16,48},{24,56},{32,64},{40,72},{48,80},{56,88},{64,... | collective-permute-start | bytes 2211848 | tf_op jit(solution)/shard_map/ppermute | solution.py:28
  8.8 18.3 %collective-permute-start.22 = (bf16[576,640]{1,0:T(8,128)(2,1)S(1)}, bf16[576,640]{1,0:T(8,128)(2,1)S(1)}, u32[]{:S(2)}, u32[]{:S(2)}) collective-permute-start(bf16[576,640]{1,0:T(8,128)(2,1)S(1)} %pad_maximum_fusion.1.refs_0_), channel_id=1, source_target_pairs={{0,16},{8,24},{16,0},{24,8},{32,48},{40,56},{48,32},{56,40},{64,80... | collective-permute-start | bytes 2211848 | tf_op jit(solution)/shard_map/ppermute | solution.py:28
  14.4 4.5 %collective-permute-start = (bf16[320,320]{1,0:T(8,128)(2,1)}, bf16[320,320]{1,0:T(8,128)(2,1)}, u32[]{:S(2)}, u32[]{:S(2)}) collective-permute-start(bf16[320,320]{1,0:T(8,128)(2,1)} %constant_dynamic-slice_fusion), channel_id=1, source_target_pairs={{0,8},{8,0},{16,24},{24,16},{32,40},{40,32},{48,56},{56,48},{64,72... | collective-permute-start | bytes 614408 | tf_op jit(solution)/shard_map/ppermute | solution.py:28
  31.1 33.8 %collective-permute-start.23 = (bf16[3008,640]{1,0:T(8,128)(2,1)S(1)}, bf16[3008,640]{1,0:T(8,128)(2,1)S(1)}, u32[]{:S(2)}, u32[]{:S(2)}) collective-permute-start(bf16[3008,640]{1,0:T(8,128)(2,1)S(1)} %get-tuple-element.28), channel_id=1, source_target_pairs={{0,8},{8,0},{16,24},{24,16},{32,40},{40,32},{48,56},{56,48},{64,72... | collective-permute-start | bytes 11550728 | tf_op jit(solution)/shard_map/ppermute | solution.py:28
  33.0 21.5 %collective-permute-start.1 = (bf16[704,640]{1,0:T(8,128)(2,1)S(1)}, bf16[704,640]{1,0:T(8,128)(2,1)S(1)}, u32[]{:S(2)}, u32[]{:S(2)}) collective-permute-start(bf16[704,640]{1,0:T(8,128)(2,1)S(1)} %pad_maximum_fusion.refs_1_), channel_id=1, source_target_pairs={{0,16},{8,24},{16,0},{24,8},{32,48},{40,56},{48,32},{56,40},{64,80... | collective-permute-start | bytes 2703368 | tf_op jit(solution)/shard_map/ppermute | solution.py:28
  34.2 22.4 %collective-permute-start.18 = (bf16[704,640]{1,0:T(8,128)(2,1)S(1)}, bf16[704,640]{1,0:T(8,128)(2,1)S(1)}, u32[]{:S(2)}, u32[]{:S(2)}) collective-permute-start(bf16[704,640]{1,0:T(8,128)(2,1)S(1)} %pad_maximum_fusion.refs_1_), channel_id=1, source_target_pairs={{0,32},{8,40},{16,48},{24,56},{32,64},{40,72},{48,80},{56,88},{64,... | collective-permute-start | bytes 2703368 | tf_op jit(solution)/shard_map/ppermute | solution.py:28
  34.2 22.4 %collective-permute-start.20 = (bf16[704,640]{1,0:T(8,128)(2,1)S(1)}, bf16[704,640]{1,0:T(8,128)(2,1)S(1)}, u32[]{:S(2)}, u32[]{:S(2)}) collective-permute-start(bf16[704,640]{1,0:T(8,128)(2,1)S(1)} %pad_maximum_fusion.refs_1_), channel_id=1, source_target_pairs={{0,96},{8,104},{16,112},{24,120},{32,0},{40,8},{48,16},{56,24},{64... | collective-permute-start | bytes 2703368 | tf_op jit(solution)/shard_map/ppermute | solution.py:28
  36.9 26.6 %collective-permute-start.13 = (bf16[288,640]{1,0:T(8,128)(2,1)S(1)}, bf16[288,640]{1,0:T(8,128)(2,1)S(1)}, u32[]{:S(2)}, u32[]{:S(2)}) collective-permute-start(bf16[288,640]{1,0:T(8,128)(2,1)S(1)} %slice.47), channel_id=1, source_target_pairs={{0,96},{8,104},{16,112},{24,120},{32,0},{40,8},{48,16},{56,24},{64... | collective-permute-start | bytes 1105928 | tf_op jit(solution)/shard_map/ppermute | solution.py:28
  54.5 10.4 %collective-permute-start.9 = (bf16[288,640]{1,0:T(8,128)(2,1)S(1)}, bf16[288,640]{1,0:T(8,128)(2,1)S(1)}, u32[]{:S(2)}, u32[]{:S(2)}) collective-permute-start(bf16[288,640]{1,0:T(8,128)(2,1)S(1)} %slice.46), channel_id=1, source_target_pairs={{0,32},{8,40},{16,48},{24,56},{32,64},{40,72},{48,80},{56,88},{64,... | collective-permute-start | bytes 1105928 | tf_op jit(solution)/shard_map/ppermute | solution.py:28
  69.6 46.6 %collective-permute-start.24 = (bf16[2688,640]{1,0:T(8,128)(2,1)S(1)}, bf16[2688,640]{1,0:T(8,128)(2,1)S(1)}, u32[]{:S(2)}, u32[]{:S(2)}) collective-permute-start(bf16[2688,640]{1,0:T(8,128)(2,1)S(1)} %get-tuple-element.33), channel_id=1, source_target_pairs={{0,8},{8,0},{16,24},{24,16},{32,40},{40,32},{48,56},{56,48},{64,72... | collective-permute-start | bytes 10321928 | tf_op jit(solution)/shard_map/ppermute | solution.py:28
  71.5 18.0 %collective-permute-start.16 = (bf16[576,640]{1,0:T(8,128)(2,1)S(1)}, bf16[576,640]{1,0:T(8,128)(2,1)S(1)}, u32[]{:S(2)}, u32[]{:S(2)}) collective-permute-start(bf16[576,640]{1,0:T(8,128)(2,1)S(1)} %collective-permute-done.8.refs_2_), channel_id=1, source_target_pairs={{0,16},{8,24},{16,0},{24,8},{32,48},{40,56},{48,32},{56,40},{64,80... | collective-permute-start | bytes 2211848 | tf_op jit(solution)/shard_map/ppermute | solution.py:28
  72.7 32.5 %collective-permute-start.17 = (bf16[576,640]{1,0:T(8,128)(2,1)S(1)}, bf16[576,640]{1,0:T(8,128)(2,1)S(1)}, u32[]{:S(2)}, u32[]{:S(2)}) collective-permute-start(bf16[576,640]{1,0:T(8,128)(2,1)S(1)} %collective-permute-done.12.refs_3_), channel_id=1, source_target_pairs={{0,16},{8,24},{16,0},{24,8},{32,48},{40,56},{48,32},{56,40},{64,80... | collective-permute-start | bytes 2211848 | tf_op jit(solution)/shard_map/ppermute | solution.py:28
  73.0 43.2 %collective-permute-start.2 = (bf16[704,640]{1,0:T(8,128)(2,1)S(1)}, bf16[704,640]{1,0:T(8,128)(2,1)S(1)}, u32[]{:S(2)}, u32[]{:S(2)}) collective-permute-start(bf16[704,640]{1,0:T(8,128)(2,1)S(1)} %collective-permute-done.1.refs_2_), channel_id=1, source_target_pairs={{0,32},{8,40},{16,48},{24,56},{32,64},{40,72},{48,80},{56,88},{64,... | collective-permute-start | bytes 2703368 | tf_op jit(solution)/shard_map/ppermute | solution.py:28
  73.0 43.2 %collective-permute-start.5 = (bf16[704,640]{1,0:T(8,128)(2,1)S(1)}, bf16[704,640]{1,0:T(8,128)(2,1)S(1)}, u32[]{:S(2)}, u32[]{:S(2)}) collective-permute-start(bf16[704,640]{1,0:T(8,128)(2,1)S(1)} %collective-permute-done.1.refs_2_), channel_id=1, source_target_pairs={{0,96},{8,104},{16,112},{24,120},{32,0},{40,8},{48,16},{56,24},{64... | collective-permute-start | bytes 2703368 | tf_op jit(solution)/shard_map/ppermute | solution.py:28
  89.5 17.5 %collective-permute-start.19 = (bf16[352,640]{1,0:T(8,128)(2,1)S(1)}, bf16[352,640]{1,0:T(8,128)(2,1)S(1)}, u32[]{:S(2)}, u32[]{:S(2)}) collective-permute-start(bf16[352,640]{1,0:T(8,128)(2,1)S(1)} %slice.48), channel_id=1, source_target_pairs={{0,32},{8,40},{16,48},{24,56},{32,64},{40,72},{48,80},{56,88},{64,... | collective-permute-start | bytes 1351688 | tf_op jit(solution)/shard_map/ppermute | solution.py:28
  105.3 11.0 %collective-permute-start.21 = (bf16[352,640]{1,0:T(8,128)(2,1)S(1)}, bf16[352,640]{1,0:T(8,128)(2,1)S(1)}, u32[]{:S(2)}, u32[]{:S(2)}) collective-permute-start(bf16[352,640]{1,0:T(8,128)(2,1)S(1)} %slice.49), channel_id=1, source_target_pairs={{0,96},{8,104},{16,112},{24,120},{32,0},{40,8},{48,16},{56,24},{64... | collective-permute-start | bytes 1351688 | tf_op jit(solution)/shard_map/ppermute | solution.py:28
  123.7 46.3 %collective-permute-start.25 = (bf16[3264,640]{1,0:T(8,128)(2,1)}, bf16[3264,640]{1,0:T(8,128)(2,1)}, u32[]{:S(2)}, u32[]{:S(2)}) collective-permute-start(bf16[3264,640]{1,0:T(8,128)(2,1)} %get-tuple-element.38), channel_id=1, source_target_pairs={{0,8},{8,0},{16,24},{24,16},{32,40},{40,32},{48,56},{56,48},{64,72... | collective-permute-start | bytes 12533768 | tf_op jit(solution)/shard_map/ppermute | solution.py:28
  125.6 29.2 %collective-permute-start.3 = (bf16[352,640]{1,0:T(8,128)(2,1)S(1)}, bf16[352,640]{1,0:T(8,128)(2,1)S(1)}, u32[]{:S(2)}, u32[]{:S(2)}) collective-permute-start(bf16[352,640]{1,0:T(8,128)(2,1)S(1)} %slice.44), channel_id=1, source_target_pairs={{0,32},{8,40},{16,48},{24,56},{32,64},{40,72},{48,80},{56,88},{64,... | collective-permute-start | bytes 1351688 | tf_op jit(solution)/shard_map/ppermute | solution.py:28
  125.8 33.1 %collective-permute-start.6 = (bf16[352,640]{1,0:T(8,128)(2,1)S(1)}, bf16[352,640]{1,0:T(8,128)(2,1)S(1)}, u32[]{:S(2)}, u32[]{:S(2)}) collective-permute-start(bf16[352,640]{1,0:T(8,128)(2,1)S(1)} %slice.45), channel_id=1, source_target_pairs={{0,96},{8,104},{16,112},{24,120},{32,0},{40,8},{48,16},{56,24},{64... | collective-permute-start | bytes 1351688 | tf_op jit(solution)/shard_map/ppermute | solution.py:28
  128.8 4.0 %collective-permute-start.26 = (bf16[1,128]{1,0:T(2,128)(2,1)S(1)}, bf16[1,128]{1,0:T(2,128)(2,1)S(1)}, u32[]{:S(2)}, u32[]{:S(2)}) collective-permute-start(bf16[1,128]{1,0:T(2,128)(2,1)S(1)} %pad_bitcast_fusion), channel_id=1, source_target_pairs={{0,2},{1,3},{2,4},{3,5},{4,6},{5,7},{6,0},{7,1},{8,10},{9,11},{10,... | collective-permute-start | bytes 776 | tf_op jit(solution)/shard_map/ppermute | solution.py:28
  130.1 4.2 %collective-permute-start.27 = (bf16[1,128]{1,0:T(2,128)(2,1)S(1)}, bf16[1,128]{1,0:T(2,128)(2,1)S(1)}, u32[]{:S(2)}, u32[]{:S(2)}) collective-permute-start(bf16[1,128]{1,0:T(2,128)(2,1)S(1)} %pad_bitcast_fusion), channel_id=1, source_target_pairs={{0,4},{1,5},{2,6},{3,7},{4,0},{5,1},{6,2},{7,3},{8,12},{9,13},{10,... | collective-permute-start | bytes 776 | tf_op jit(solution)/shard_map/ppermute | solution.py:28
  135.5 4.0 %collective-permute-start.29 = (bf16[4,128]{1,0:T(4,128)(2,1)S(1)}, bf16[4,128]{1,0:T(4,128)(2,1)S(1)}, u32[]{:S(2)}, u32[]{:S(2)}) collective-permute-start(bf16[4,128]{1,0:T(4,128)(2,1)S(1)} %pad_maximum_fusion.2), channel_id=1, source_target_pairs={{0,1},{1,0},{2,3},{3,2},{4,5},{5,4},{6,7},{7,6},{8,9},{9,8},{10,11... | collective-permute-start | bytes 3080 | tf_op jit(solution)/shard_map/ppermute | solution.py:28
  139.5 4.0 %collective-permute-start.30 = (bf16[8,128]{1,0:T(8,128)(2,1)S(1)}, bf16[8,128]{1,0:T(8,128)(2,1)S(1)}, u32[]{:S(2)}, u32[]{:S(2)}) collective-permute-start(bf16[8,128]{1,0:T(8,128)(2,1)S(1)} %concatenate.32), channel_id=1, source_target_pairs={{0,8},{8,0},{16,24},{24,16},{32,40},{40,32},{48,56},{56,48},{64,72... | collective-permute-start | bytes 6152 | tf_op jit(solution)/shard_map/ppermute | solution.py:28
  146.2 3.8 %collective-permute-start.32 = (bf16[32,128]{1,0:T(8,128)(2,1)S(1)}, bf16[32,128]{1,0:T(8,128)(2,1)S(1)}, u32[]{:S(2)}, u32[]{:S(2)}) collective-permute-start(bf16[32,128]{1,0:T(8,128)(2,1)S(1)} %concatenate.34), channel_id=1, source_target_pairs={{0,32},{8,40},{16,48},{24,56},{32,64},{40,72},{48,80},{56,88},{64,... | collective-permute-start | bytes 24584 | tf_op jit(solution)/shard_map/ppermute | solution.py:28
  149.9 3.7 %collective-permute-start.33 = (bf16[32,128]{1,0:T(8,128)(2,1)S(1)}, bf16[32,128]{1,0:T(8,128)(2,1)S(1)}, u32[]{:S(2)}, u32[]{:S(2)}) collective-permute-start(bf16[32,128]{1,0:T(8,128)(2,1)S(1)} %collective-permute-done.32), channel_id=1, source_target_pairs={{0,32},{8,40},{16,48},{24,56},{32,64},{40,72},{48,80},{56,88},{64,... | collective-permute-start | bytes 24584 | tf_op jit(solution)/shard_map/ppermute | solution.py:28
  149.9 9.1 %collective-permute-start.10 = (bf16[288,640]{1,0:T(8,128)(2,1)S(1)}, bf16[288,640]{1,0:T(8,128)(2,1)S(1)}, u32[]{:S(2)}, u32[]{:S(2)}) collective-permute-start(bf16[288,640]{1,0:T(8,128)(2,1)S(1)} %collective-permute-done.9.refs_3_), channel_id=1, source_target_pairs={{0,16},{8,24},{16,0},{24,8},{32,48},{40,56},{48,32},{56,40},{64,80... | collective-permute-start | bytes 1105928 | tf_op jit(solution)/shard_map/ppermute | solution.py:28
  153.6 11.7 %collective-permute-start.14 = (bf16[288,640]{1,0:T(8,128)(2,1)S(1)}, bf16[288,640]{1,0:T(8,128)(2,1)S(1)}, u32[]{:S(2)}, u32[]{:S(2)}) collective-permute-start(bf16[288,640]{1,0:T(8,128)(2,1)S(1)} %collective-permute-done.13.refs_4_), channel_id=1, source_target_pairs={{0,16},{8,24},{16,0},{24,8},{32,48},{40,56},{48,32},{56,40},{64,80... | collective-permute-start | bytes 1105928 | tf_op jit(solution)/shard_map/ppermute | solution.py:28
  154.8 21.0 %collective-permute-start.4 = (bf16[352,640]{1,0:T(8,128)(2,1)S(1)}, bf16[352,640]{1,0:T(8,128)(2,1)S(1)}, u32[]{:S(2)}, u32[]{:S(2)}) collective-permute-start(bf16[352,640]{1,0:T(8,128)(2,1)S(1)} %collective-permute-done.3.refs_0_), channel_id=1, source_target_pairs={{0,8},{8,0},{16,24},{24,16},{32,40},{40,32},{48,56},{56,48},{64,72... | collective-permute-start | bytes 1351688 | tf_op jit(solution)/shard_map/ppermute | solution.py:28
  158.9 17.0 %collective-permute-start.7 = (bf16[352,640]{1,0:T(8,128)(2,1)S(1)}, bf16[352,640]{1,0:T(8,128)(2,1)S(1)}, u32[]{:S(2)}, u32[]{:S(2)}) collective-permute-start(bf16[352,640]{1,0:T(8,128)(2,1)S(1)} %collective-permute-done.6.refs_1_), channel_id=1, source_target_pairs={{0,8},{8,0},{16,24},{24,16},{32,40},{40,32},{48,56},{56,48},{64,72... | collective-permute-start | bytes 1351688 | tf_op jit(solution)/shard_map/ppermute | solution.py:28
  159.0 16.9 %collective-permute-start.11 = (bf16[288,640]{1,0:T(8,128)(2,1)S(1)}, bf16[288,640]{1,0:T(8,128)(2,1)S(1)}, u32[]{:S(2)}, u32[]{:S(2)}) collective-permute-start(bf16[288,640]{1,0:T(8,128)(2,1)S(1)} %collective-permute-done.10.refs_2_), channel_id=1, source_target_pairs={{0,8},{8,0},{16,24},{24,16},{32,40},{40,32},{48,56},{56,48},{64,72... | collective-permute-start | bytes 1105928 | tf_op jit(solution)/shard_map/ppermute | solution.py:28
  165.3 10.5 %collective-permute-start.15 = (bf16[288,640]{1,0:T(8,128)(2,1)S(1)}, bf16[288,640]{1,0:T(8,128)(2,1)S(1)}, u32[]{:S(2)}, u32[]{:S(2)}) collective-permute-start(bf16[288,640]{1,0:T(8,128)(2,1)S(1)} %collective-permute-done.14.refs_3_), channel_id=1, source_target_pairs={{0,8},{8,0},{16,24},{24,16},{32,40},{40,32},{48,56},{56,48},{64,72... | collective-permute-start | bytes 1105928 | tf_op jit(solution)/shard_map/ppermute | solution.py:28
  (10 other events, 75.3 us)
where the time goes:
time: 178 us
  waiting for transfers between devices  82 us (46%)
  starting transfers between devices  56.1 us (32%)
  Pallas kernels  23.8 us (13%)
  matrix products  7.52 us (4%)
  local copies, waits for them, and re-layouts  4.97 us (3%)
  other arithmetic  2.37 us (1%)
    ppermute x35, waiting for transfers between devices, send(): return lax.ppermute(a, axis, perm)  82 us
    ppermute x35, starting transfers between devices, send(): return lax.ppermute(a, axis, perm)  56.1 us
    pallas_call x5, Pallas kernels, assemble(): result = call(place, *[v for _, v in own], *[v for _, v in other], *before)  23.8 us
    dot_general x5, matrix products, updated(): product = jnp.dot(low, high, preferred_element_type=jnp.float32)  7.32 us
  transfers between devices with their start and end apart: 35, of which 17 were waited for; matrix products, arithmetic and copies ran while one was open for 6% of the time, Pallas kernels for 3%

commit v1 on v0

--- a/solution.py
+++ b/solution.py
@@ -13,15 +13,17 @@
 B_ROWS = BLOCK + HEAD
 A_ROWS = 3 * BLOCK - HEAD
 
-Z_UP = [(f, (f + 4) % 16) for f in range(16)]
-Z_DOWN = [(f, (f - 4) % 16) for f in range(16)]
 X_SWAP = [(f, f ^ 2) for f in range(16)]
 CORE_SWAP = [(f, f ^ 1) for f in range(16)]
 HI_SWAP = [(k, k ^ 1) for k in range(8)]
 
 
-def y_up(s):
+def y_by(s):
     return [(k, (k + 2 * s) % 8) for k in range(8)]
+
+
+def z_by(s):
+    return [(f, (f + 4 * s) % 16) for f in range(16)]
 
 
 def send(a, perm, axis="fsdp"):
@@ -63,14 +65,15 @@
     return found
 
 
-def assemble(place, own, other, outs, stack=True):
+def assemble(place, own, other, outs, stack=True, extra=None):
     n_own, n_other = len(own), len(other)
     rows = sum(rows_of(p) for p, _ in own)
     before = [] if outs is None else list(outs)
+    extras = [] if extra is None else [extra]
 
     def body(place_ref, *refs):
         own_refs, other_refs = refs[:n_own], refs[n_own : n_own + n_other]
-        refs = refs[n_own + n_other + len(before) :]
+        refs = refs[n_own + n_other + len(before) + len(extras) :]
         out_refs, refs = refs[:4], refs[4:]
         stack_ref, load_sem, store_sem = refs if own else (None, None, refs[0])
         where = (place_ref[0], place_ref[1], place_ref[2])
@@ -118,30 +121,31 @@
     call = pl.pallas_call(
         body,
         out_shape=shapes,
-        in_specs=[pl.BlockSpec(memory_space=pltpu.SMEM)] + [any_spec] * n_own + [vmem_spec] * n_other + [any_spec] * len(before),
+        in_specs=[pl.BlockSpec(memory_space=pltpu.SMEM)] + [any_spec] * n_own + [vmem_spec] * n_other + [any_spec] * (len(before) + len(extras)),
         out_specs=out_specs,
         scratch_shapes=scratch,
         input_output_aliases={1 + n_own + n_other + i: i for i in range(len(before))},
         compiler_params=pltpu.CompilerParams(vmem_limit_bytes=12 << 20),
     )
-    result = call(place, *[v for _, v in own], *[v for _, v in other], *before)
+    result = call(place, *[v for _, v in own], *[v for _, v in other], *before, *extras)
     return result[:4], (result[4] if own and stack else None)
 
 
 def gathered_norm(norm_train, norm_step, z, x, c):
     mine = (norm_train + norm_step).astype(jnp.bfloat16)
     rows = jnp.pad(mine, (0, 88))[None, :]
-    rows = jnp.concatenate([rows] + [send(rows, y_up(s), "cols") for s in (1, 2, 3)], 0)
+    rows = jnp.concatenate([rows, send(rows, CORE_SWAP)], 0)
+    across = send(rows, X_SWAP)
+    rows = jnp.concatenate([rows, across], 0)
+    others = [send(rows, z_by(s)) for s in (1, 2, 3)]
+    rows = jnp.concatenate([rows] + others, 0)
+    rows = jnp.concatenate([rows] + [send(rows, y_by(s), "cols") for s in (1, 2, 3)], 0)
     rows = jnp.concatenate([rows, send(rows, HI_SWAP, "cols")], 0)
-    rows = jnp.concatenate([rows, send(rows, CORE_SWAP)], 0)
-    rows = jnp.concatenate([rows, send(rows, X_SWAP)], 0)
-    below = send(rows, Z_UP)
-    rows = jnp.concatenate([rows, below, send(below, Z_UP), send(rows, Z_DOWN)], 0)
     k = lax.axis_index("cols")
     y, hi = k // 2, k % 2
     r = lax.iota(jnp.int32, 128)
-    col = ((y - r % 4) % 4) * 2 + (hi ^ (r // 4 % 2))
-    part = ((z - r // 32) % 4) * 4 + (x ^ (r // 16 % 2)) * 2 + (c ^ (r // 8 % 2))
+    part = ((z - r // 4 % 4) % 4) * 4 + (x ^ (r // 2 % 2)) * 2 + (c ^ (r % 2))
+    col = ((y - r // 16 % 4) % 4) * 2 + (hi ^ (r // 64))
     place = (lax.iota(jnp.int32, 128)[:, None] == (part * 8 + col)[None, :]).astype(jnp.bfloat16)
     ordered = jnp.dot(place, rows, preferred_element_type=jnp.float32).astype(jnp.bfloat16)
     return ordered[:, :40].reshape(5120)
@@ -181,14 +185,14 @@
     )
 
     hb, ha = B_ROWS // 2, A_ROWS // 2
-    b_up, b_down, b_x = send(b, Z_UP), send(b, Z_DOWN), send(b, X_SWAP)
-    a_up, a_down, a_x = send(a, Z_UP), send(a, Z_DOWN), send(a, X_SWAP)
-    b_up2, b_down2 = send(b_up[:hb], Z_UP), send(b_down[hb:], Z_DOWN)
+    b_up, b_down, b_x = send(b, z_by(1)), send(b, z_by(3)), send(b, X_SWAP)
+    a_up, a_down, a_x = send(a, z_by(1)), send(a, z_by(3)), send(a, X_SWAP)
+    b_up2, b_down2 = send(b_up[:hb], z_by(1)), send(b_down[hb:], z_by(3))
     bx_up, bx_down = send(b_up, X_SWAP), send(b_down, X_SWAP)
-    ax_up, ax_down = send(a_x, Z_UP), send(a_x, Z_DOWN)
-    a_up2, a_down2 = send(a_up[:ha], Z_UP), send(a_down[ha:], Z_DOWN)
+    ax_up, ax_down = send(a_x, z_by(1)), send(a_x, z_by(3))
+    a_up2, a_down2 = send(a_up[:ha], z_by(1)), send(a_down[ha:], z_by(3))
     bx_up2, bx_down2 = send(b_up2, X_SWAP), send(b_down2, X_SWAP)
-    ax_up2, ax_down2 = send(ax_up[:ha], Z_UP), send(ax_down[ha:], Z_DOWN)
+    ax_up2, ax_down2 = send(ax_up[:ha], z_by(1)), send(ax_down[ha:], z_by(3))
 
     serve_norm = gathered_norm(norm_train, norm_step, z, x, c)
 
@@ -208,12 +212,15 @@
     outs, stack1 = assemble(place, own1, [], None)
     own2 = [whole("a", 1, 0, a_up), whole("a", 3, 0, a_down), whole("a", 0, 1, a_x), top("b", 0, b_up2), bottom("b", 0, b_down2)]
     outs, stack2 = assemble(place, own2, [swapped(own1, stack1)], outs)
-    own3 = [whole("a", 1, 1, ax_up), whole("a", 3, 1, ax_down), whole("b", 1, 1, bx_up), whole("b", 3, 1, bx_down), top("a", 0, a_up2), bottom("a", 0, a_down2)]
+    own3 = [whole("a", 1, 1, ax_up), whole("a", 3, 1, ax_down), whole("b", 1, 1, bx_up)]
     outs, stack3 = assemble(place, own3, [swapped(own2, stack2)], outs)
-    own4 = [top("a", 1, ax_up2), bottom("a", 1, ax_down2), top("b", 1, bx_up2), bottom("b", 1, bx_down2)]
+    own4 = [whole("b", 3, 1, bx_down), top("a", 0, a_up2), bottom("a", 0, a_down2)]
     late = [([p], send(v, CORE_SWAP)) for p, v in own4]
-    outs, _ = assemble(place, own4, [swapped(own3, stack3)], outs, stack=False)
-    outs, _ = assemble(place, [], late, outs)
+    outs, _ = assemble(place, own4, [swapped(own3, stack3)], outs, stack=False, extra=serve_norm)
+    own5 = [top("b", 1, bx_up2), bottom("b", 1, bx_down2), top("a", 1, ax_up2), bottom("a", 1, ax_down2)]
+    last = [([p], send(v, CORE_SWAP)) for p, v in own5]
+    outs, _ = assemble(place, own5, late, outs, stack=False)
+    outs, _ = assemble(place, [], last, outs)
     return (*outs, serve_norm)
 
 

time: 178 us -> 178 us (level)
  waiting for transfers between devices: 82 us -> 71.6 us
  local copies, waits for them, and re-layouts: 4.97 us -> 10.9 us
  starting transfers between devices: 56.1 us -> 60.6 us
    ppermute x35 -> x38, waiting for transfers between devices: 82 us -> 71.6 us  [send(): return lax.ppermute(a, axis, perm)]
    ppermute x35 -> x38, starting transfers between devices: 56.1 us -> 60.6 us  [send(): return lax.ppermute(a, axis, perm)]
    slice x6, local copies, waits for them, and re-layouts: 0.23 us -> 4.06 us  [the longest x2 2.11 us: per_device(): ax_up2, ax_down2 = (send(ax_up[:ha], z_by(1)), send(ax_down[ha:], z_by(3)))]
    unnamed x14 -> x44, local copies, waits for them, and re-layouts: 0.79 us -> 4.2 us
    pallas_call x5 -> x6, Pallas kernels: 23.8 us -> 23.7 us  [assemble(): call(place, *[v for _, v in own], *[v for _, v in other], *before, *extras)]
  transfers between devices with their start and end apart: 35 -> 38, of which waited for: 17 -> 14; matrix products, arithmetic and copies ran while one was open for 6% -> 7% of each run, Pallas kernels for 3% -> 4%
where the time goes in v1:
time: 178 us; the launch traced here: 177 us
  waiting for transfers between devices  71.6 us (40%)
  starting transfers between devices  60.6 us (34%)
  Pallas kernels  23.7 us (13%)
  local copies, waits for them, and re-layouts  10.9 us (6%)
  matrix products  6.52 us (4%)
  other arithmetic  2.38 us (1%)
    ppermute x38, waiting for transfers between devices, send(): return lax.ppermute(a, axis, perm)  71.6 us
    ppermute x38, starting transfers between devices, send(): return lax.ppermute(a, axis, perm)  60.6 us
    pallas_call x6, Pallas kernels, assemble(): call(place, *[v for _, v in own], *[v for _, v in other], *before, *extras)  23.7 us
    dot_general x5, matrix products, updated(): product = jnp.dot(low, high, preferred_element_type=jnp.float32)  6.31 us
    unnamed x44, local copies, waits for them, and re-layouts  4.2 us
  transfers between devices with their start and end apart: 38, of which 14 were waited for; matrix products, arithmetic and copies ran while one was open for 7% of the time, Pallas kernels for 4%

profile of v1, /device:TPU:1, one launch (start us, length us, event | category | flops | bytes accessed | tf_op | source)
XLA Modules:
  0.0 177.0 jit_solution(4799346839757970381)
XLA Ops:
  4.1 2.5 %collective-permute-start = (bf16[576,640]{1,0:T(8,128)(2,1)S(1)}, bf16[576,640]{1,0:T(8,128)(2,1)S(1)}, u32[]{:S(2)}, u32[]{:S(2)}) collective-permute-start(bf16[576,640]{1,0:T(8,128)(2,1)S(1)} %pad_maximum_fusion.1.refs_0_), channel_id=1, source_target_pairs={{0,32},{8,40},{16,48},{24,56},{32,64},{40,72},{48,80},{56,88},{64,... | collective-permute-start | bytes 2211848 | tf_op jit(solution)/shard_map/ppermute | solution.py:30
  6.6 2.2 %collective-permute-start.4 = (bf16[576,640]{1,0:T(8,128)(2,1)S(1)}, bf16[576,640]{1,0:T(8,128)(2,1)S(1)}, u32[]{:S(2)}, u32[]{:S(2)}) collective-permute-start(bf16[576,640]{1,0:T(8,128)(2,1)S(1)} %pad_maximum_fusion.1.refs_0_), channel_id=1, source_target_pairs={{0,96},{8,104},{16,112},{24,120},{32,0},{40,8},{48,16},{56,24},{64... | collective-permute-start | bytes 2211848 | tf_op jit(solution)/shard_map/ppermute | solution.py:30
  10.0 2.1 %copy.45 = f32[640,320]{1,0:T(8,128)} copy(bf16[640,320]{0,1:T(8,128)(2,1)} %param.23) | data formatting | bytes 1228800 | tf_op jit(solution)/shard_map/convert_element_type | solution.py:35
  12.2 1.6 fusion.3
  19.6 5.4 %collective-permute-done.refs_2_ = bf16[576,640]{1,0:T(8,128)(2,1)S(1)} collective-permute-done((bf16[576,640]{1,0:T(8,128)(2,1)S(1)}, bf16[576,640]{1,0:T(8,128)(2,1)S(1)}, u32[]{:S(2)}, u32[]{:S(2)}) %collective-permute-start) | collective-permute-done | bytes 737312 | tf_op jit(solution)/shard_map/ppermute | solution.py:30
  26.0 4.3 %shard_map.173 = (bf16[5120,640]{1,0:T(8,128)(2,1)}, bf16[5120,640]{1,0:T(8,128)(2,1)}, bf16[5120,640]{1,0:T(8,128)(2,1)}, bf16[640,5120]{1,0:T(8,128)(2,1)}, bf16[3008,640]{1,0:T(8,128)(2,1)S(1)}) custom-call(s32[3]{0:T(128)S(1)} %pad_add_fusion.place_ref, bf16[576,640]{1,0:T(8,128)(2,1)S(1)} %pad_maximum_fusion.1.refs_0_, ...), custom_call_target="tpu_custom_call" | custom-call | tf_op jit(solution)/shard_map/pallas_call | solution.py:130
  30.4 1.9 %collective-permute-start.26 = (bf16[3008,640]{1,0:T(8,128)(2,1)S(1)}, bf16[3008,640]{1,0:T(8,128)(2,1)S(1)}, u32[]{:S(2)}, u32[]{:S(2)}) collective-permute-start(bf16[3008,640]{1,0:T(8,128)(2,1)S(1)} %get-tuple-element.32), channel_id=1, source_target_pairs={{0,8},{8,0},{16,24},{24,16},{32,40},{40,32},{48,56},{56,48},{64,72... | collective-permute-start | bytes 11550728 | tf_op jit(solution)/shard_map/ppermute | solution.py:30
  32.3 2.7 %collective-permute-start.21 = (bf16[704,640]{1,0:T(8,128)(2,1)S(1)}, bf16[704,640]{1,0:T(8,128)(2,1)S(1)}, u32[]{:S(2)}, u32[]{:S(2)}) collective-permute-start(bf16[704,640]{1,0:T(8,128)(2,1)S(1)} %pad_maximum_fusion.refs_1_), channel_id=1, source_target_pairs={{0,96},{8,104},{16,112},{24,120},{32,0},{40,8},{48,16},{56,24},{64... | collective-permute-start | bytes 2703368 | tf_op jit(solution)/shard_map/ppermute | solution.py:30
  37.3 17.6 %collective-permute-done.18.refs_0_ = bf16[704,640]{1,0:T(8,128)(2,1)S(1)} collective-permute-done((bf16[704,640]{1,0:T(8,128)(2,1)S(1)}, bf16[704,640]{1,0:T(8,128)(2,1)S(1)}, u32[]{:S(2)}, u32[]{:S(2)}) %collective-permute-start.18) | collective-permute-done | bytes 901152 | tf_op jit(solution)/shard_map/ppermute | solution.py:30
  55.8 7.0 %collective-permute-done.1.refs_3_ = bf16[288,640]{1,0:T(8,128)(2,1)S(1)} collective-permute-done((bf16[288,640]{1,0:T(8,128)(2,1)S(1)}, bf16[288,640]{1,0:T(8,128)(2,1)S(1)}, u32[]{:S(2)}, u32[]{:S(2)}) %collective-permute-start.1) | collective-permute-done | bytes 368672 | tf_op jit(solution)/shard_map/ppermute | solution.py:30
  63.6 4.7 %shard_map.174 = (bf16[5120,640]{1,0:T(8,128)(2,1)}, bf16[5120,640]{1,0:T(8,128)(2,1)}, bf16[5120,640]{1,0:T(8,128)(2,1)}, bf16[640,5120]{1,0:T(8,128)(2,1)}, bf16[2688,640]{1,0:T(8,128)(2,1)S(1)}) custom-call(s32[3]{0:T(128)S(1)} %pad_add_fusion.place_ref, ...), custom_call_target="tpu_custom_call", output_to_operand_aliasing={{0}: (7, {}), {1}: (8, {}), {2}: (9, {}), {3}: (10, {})} | custom-call | tf_op jit(solution)/shard_map/pallas_call | solution.py:130
  68.3 2.4 %collective-permute-start.27 = (bf16[2688,640]{1,0:T(8,128)(2,1)S(1)}, bf16[2688,640]{1,0:T(8,128)(2,1)S(1)}, u32[]{:S(2)}, u32[]{:S(2)}) collective-permute-start(bf16[2688,640]{1,0:T(8,128)(2,1)S(1)} %get-tuple-element.37), channel_id=1, source_target_pairs={{0,8},{8,0},{16,24},{24,16},{32,40},{40,32},{48,56},{56,48},{64,72... | collective-permute-start | bytes 10321928 | tf_op jit(solution)/shard_map/ppermute | solution.py:30
  70.8 2.7 %collective-permute-start.13 = (bf16[704,640]{1,0:T(8,128)(2,1)S(1)}, bf16[704,640]{1,0:T(8,128)(2,1)S(1)}, u32[]{:S(2)}, u32[]{:S(2)}) collective-permute-start(bf16[704,640]{1,0:T(8,128)(2,1)S(1)} %collective-permute-done.9.refs_2_), channel_id=1, source_target_pairs={{0,96},{8,104},{16,112},{24,120},{32,0},{40,8},{48,16},{56,24},{64... | collective-permute-start | bytes 2703368 | tf_op jit(solution)/shard_map/ppermute | solution.py:30
  74.7 16.2 %collective-permute-done.24.refs_2_ = bf16[576,640]{1,0:T(8,128)(2,1)S(1)} collective-permute-done((bf16[576,640]{1,0:T(8,128)(2,1)S(1)}, bf16[576,640]{1,0:T(8,128)(2,1)S(1)}, u32[]{:S(2)}, u32[]{:S(2)}) %collective-permute-start.24) | collective-permute-done | bytes 737312 | tf_op jit(solution)/shard_map/ppermute | solution.py:30
  90.9 2.6 %collective-permute-done.10.refs_0_ = bf16[704,640]{1,0:T(8,128)(2,1)S(1)} collective-permute-done((bf16[704,640]{1,0:T(8,128)(2,1)S(1)}, bf16[704,640]{1,0:T(8,128)(2,1)S(1)}, u32[]{:S(2)}, u32[]{:S(2)}) %collective-permute-start.10) | collective-permute-done | bytes 901152 | tf_op jit(solution)/shard_map/ppermute | solution.py:30
  93.5 5.5 %shard_map.175 = (bf16[5120,640]{1,0:T(8,128)(2,1)}, bf16[5120,640]{1,0:T(8,128)(2,1)}, bf16[5120,640]{1,0:T(8,128)(2,1)}, bf16[640,5120]{1,0:T(8,128)(2,1)}, bf16[1984,640]{1,0:T(8,128)(2,1)}) custom-call(s32[3]{0:T(128)S(1)} %pad_add_fusion.place_ref, ...), custom_call_target="tpu_custom_call", output_to_operand_aliasing={{0}: (5, {}), {1}: (6, {}), {2}: (7, {}), {3}: (8, {})} | custom-call | tf_op jit(solution)/shard_map/pallas_call | solution.py:130
  102.6 2.1 %collective-permute-done.29 = bf16[1,128]{1,0:T(2,128)(2,1)S(1)} collective-permute-done((bf16[1,128]{1,0:T(2,128)(2,1)S(1)}, bf16[1,128]{1,0:T(2,128)(2,1)S(1)}, u32[]{:S(2)}, u32[]{:S(2)}) %collective-permute-start.29) | collective-permute-done | bytes 288 | tf_op jit(solution)/shard_map/ppermute | solution.py:30
  105.9 12.4 %collective-permute-done.30 = bf16[2,128]{1,0:T(2,128)(2,1)S(1)} collective-permute-done((bf16[2,128]{1,0:T(2,128)(2,1)S(1)}, bf16[2,128]{1,0:T(2,128)(2,1)S(1)}, u32[]{:S(2)}, u32[]{:S(2)}) %collective-permute-start.30) | collective-permute-done | bytes 544 | tf_op jit(solution)/shard_map/ppermute | solution.py:30
  118.4 3.9 %collective-permute-start.32 = (bf16[4,128]{1,0:T(4,128)(2,1)S(1)}, bf16[4,128]{1,0:T(4,128)(2,1)S(1)}, u32[]{:S(2)}, u32[]{:S(2)}) collective-permute-start(bf16[4,128]{1,0:T(4,128)(2,1)S(1)} %pad_maximum_fusion.2), channel_id=1, source_target_pairs={{0,64},{8,72},{16,80},{24,88},{32,96},{40,104},{48,112},{56,120},{... | collective-permute-start | bytes 3080 | tf_op jit(solution)/shard_map/ppermute | solution.py:30
  123.5 1.4 collective-permute-done.33
  126.4 2.6 %collective-permute-start.35 = (bf16[16,128]{1,0:T(8,128)(2,1)S(1)}, bf16[16,128]{1,0:T(8,128)(2,1)S(1)}, u32[]{:S(2)}, u32[]{:S(2)}) collective-permute-start(bf16[16,128]{1,0:T(8,128)(2,1)S(1)} %concatenate.33), channel_id=1, source_target_pairs={{0,4},{1,5},{2,6},{3,7},{4,0},{5,1},{6,2},{7,3},{8,12},{9,13},{10,... | collective-permute-start | bytes 12296 | tf_op jit(solution)/shard_map/ppermute | solution.py:30
  130.3 1.4 collective-permute-done.36
  131.8 2.8 %collective-permute-start.37 = (bf16[64,128]{1,0:T(8,128)(2,1)S(1)}, bf16[64,128]{1,0:T(8,128)(2,1)S(1)}, u32[]{:S(2)}, u32[]{:S(2)}) collective-permute-start(bf16[64,128]{1,0:T(8,128)(2,1)S(1)} %concatenate.34), channel_id=1, source_target_pairs={{0,1},{1,0},{2,3},{3,2},{4,5},{5,4},{6,7},{7,6},{8,9},{9,8},{10,11... | collective-permute-start | bytes 49160 | tf_op jit(solution)/shard_map/ppermute | solution.py:30
  134.7 2.0 %collective-permute-start.22 = (bf16[352,640]{1,0:T(8,128)(2,1)S(1)}, bf16[352,640]{1,0:T(8,128)(2,1)S(1)}, u32[]{:S(2)}, u32[]{:S(2)}) collective-permute-start(bf16[352,640]{1,0:T(8,128)(2,1)S(1)} %slice.49), channel_id=1, source_target_pairs={{0,96},{8,104},{16,112},{24,120},{32,0},{40,8},{48,16},{56,24},{64... | collective-permute-start | bytes 1351688 | tf_op jit(solution)/shard_map/ppermute | solution.py:30
  138.2 6.4 %collective-permute-start.20 = (bf16[352,640]{1,0:T(8,128)(2,1)}, bf16[352,640]{1,0:T(8,128)(2,1)S(1)}, u32[]{:S(2)}, u32[]{:S(2)}) collective-permute-start(bf16[352,640]{1,0:T(8,128)(2,1)} %collective-permute-done.19.refs_1_), channel_id=1, source_target_pairs={{0,8},{8,0},{16,24},{24,16},{32,40},{40,32},{48,56},{56,48},{64,72... | collective-permute-start | bytes 1351688 | tf_op jit(solution)/shard_map/ppermute | solution.py:30
  146.8 2.8 %collective-permute-done.6.refs_1_ = bf16[288,640]{1,0:T(8,128)(2,1)} collective-permute-done((bf16[288,640]{1,0:T(8,128)(2,1)}, bf16[288,640]{1,0:T(8,128)(2,1)}, u32[]{:S(2)}, u32[]{:S(2)}) %collective-permute-start.6) | collective-permute-done | bytes 368672 | tf_op jit(solution)/shard_map/ppermute | solution.py:30
  150.0 7.6 %collective-permute-start.23 = (bf16[352,640]{1,0:T(8,128)(2,1)S(1)}, bf16[352,640]{1,0:T(8,128)(2,1)S(1)}, u32[]{:S(2)}, u32[]{:S(2)}) collective-permute-start(bf16[352,640]{1,0:T(8,128)(2,1)S(1)} %collective-permute-done.22.refs_2_), channel_id=1, source_target_pairs={{0,8},{8,0},{16,24},{24,16},{32,40},{40,32},{48,56},{56,48},{64,72... | collective-permute-start | bytes 1351688 | tf_op jit(solution)/shard_map/ppermute | solution.py:30
  159.2 2.7 %collective-permute-start.12 = (bf16[352,640]{1,0:T(8,128)(2,1)}, bf16[352,640]{1,0:T(8,128)(2,1)}, u32[]{:S(2)}, u32[]{:S(2)}) collective-permute-start(bf16[352,640]{1,0:T(8,128)(2,1)} %collective-permute-done.11.refs_2_), channel_id=1, source_target_pairs={{0,8},{8,0},{16,24},{24,16},{32,40},{40,32},{48,56},{56,48},{64,72... | collective-permute-start | bytes 1351688 | tf_op jit(solution)/shard_map/ppermute | solution.py:30
  161.8 2.7 %collective-permute-start.15 = (bf16[352,640]{1,0:T(8,128)(2,1)}, bf16[352,640]{1,0:T(8,128)(2,1)}, u32[]{:S(2)}, u32[]{:S(2)}) collective-permute-start(bf16[352,640]{1,0:T(8,128)(2,1)} %collective-permute-done.14.refs_3_), channel_id=1, source_target_pairs={{0,8},{8,0},{16,24},{24,16},{32,40},{40,32},{48,56},{56,48},{64,72... | collective-permute-start | bytes 1351688 | tf_op jit(solution)/shard_map/ppermute | solution.py:30
  167.5 3.0 %shard_map.176 = (bf16[5120,640]{1,0:T(8,128)(2,1)}, bf16[5120,640]{1,0:T(8,128)(2,1)}, bf16[5120,640]{1,0:T(8,128)(2,1)}, bf16[640,5120]{1,0:T(8,128)(2,1)}) custom-call(s32[3]{0:T(128)S(1)} %pad_add_fusion.place_ref, bf16[576,640]{1,0:T(8,128)(2,1)} %collective-permute-done.16.refs_0_, ...), custom_call_target="tpu_custom_call", output_to_operand_aliasing={{0}: (5, {}), {1}: (6, {}), {2}: (7, {}), {3}: (8, {})} | custom-call | tf_op jit(solution)/shard_map/pallas_call | solution.py:130
  170.6 3.5 %shard_map.177 = (bf16[5120,640]{1,0:T(8,128)(2,1)}, bf16[5120,640]{1,0:T(8,128)(2,1)}, bf16[5120,640]{1,0:T(8,128)(2,1)}, bf16[640,5120]{1,0:T(8,128)(2,1)}) custom-call(s32[3]{0:T(128)S(1)} %pad_add_fusion.place_ref, bf16[288,640]{1,0:T(8,128)(2,1)} %collective-permute-done.2.refs_0_, ...), custom_call_target="tpu_custom_call", output_to_operand_aliasing={{0}: (8, {}), {1}: (9, {}), {2}: (10, {}), {3}: (11, {})} | custom-call | tf_op jit(solution)/shard_map/pallas_call | solution.py:130
  174.2 2.7 %shard_map.178 = (bf16[5120,640]{1,0:T(8,128)(2,1)}, bf16[5120,640]{1,0:T(8,128)(2,1)}, bf16[5120,640]{1,0:T(8,128)(2,1)}, bf16[640,5120]{1,0:T(8,128)(2,1)}) custom-call(s32[3]{0:T(128)S(1)} %pad_add_fusion.place_ref, bf16[288,640]{1,0:T(8,128)(2,1)} %collective-permute-done.3.refs_0_, ...), custom_call_target="tpu_custom_call", output_to_operand_aliasing={{0}: (5, {}), {1}: (6, {}), {2}: (7, {}), {3}: (8, {})} | custom-call | tf_op jit(solution)/shard_map/pallas_call | solution.py:130
  (123 shorter events, 34.4 us)
Async XLA Ops:
  4.1 20.8 %collective-permute-start = (bf16[576,640]{1,0:T(8,128)(2,1)S(1)}, bf16[576,640]{1,0:T(8,128)(2,1)S(1)}, u32[]{:S(2)}, u32[]{:S(2)}) collective-permute-start(bf16[576,640]{1,0:T(8,128)(2,1)S(1)} %pad_maximum_fusion.1.refs_0_), channel_id=1, source_target_pairs={{0,32},{8,40},{16,48},{24,56},{32,64},{40,72},{48,80},{56,88},{64,... | collective-permute-start | bytes 2211848 | tf_op jit(solution)/shard_map/ppermute | solution.py:30
  6.6 18.3 %collective-permute-start.4 = (bf16[576,640]{1,0:T(8,128)(2,1)S(1)}, bf16[576,640]{1,0:T(8,128)(2,1)S(1)}, u32[]{:S(2)}, u32[]{:S(2)}) collective-permute-start(bf16[576,640]{1,0:T(8,128)(2,1)S(1)} %pad_maximum_fusion.1.refs_0_), channel_id=1, source_target_pairs={{0,96},{8,104},{16,112},{24,120},{32,0},{40,8},{48,16},{56,24},{64... | collective-permute-start | bytes 2211848 | tf_op jit(solution)/shard_map/ppermute | solution.py:30
  8.8 17.2 %collective-permute-start.25 = (bf16[576,640]{1,0:T(8,128)(2,1)S(1)}, bf16[576,640]{1,0:T(8,128)(2,1)}, u32[]{:S(2)}, u32[]{:S(2)}) collective-permute-start(bf16[576,640]{1,0:T(8,128)(2,1)S(1)} %pad_maximum_fusion.1.refs_0_), channel_id=1, source_target_pairs={{0,16},{8,24},{16,0},{24,8},{32,48},{40,56},{48,32},{56,40},{64,80... | collective-permute-start | bytes 2211848 | tf_op jit(solution)/shard_map/ppermute | solution.py:30
  30.4 33.2 %collective-permute-start.26 = (bf16[3008,640]{1,0:T(8,128)(2,1)S(1)}, bf16[3008,640]{1,0:T(8,128)(2,1)S(1)}, u32[]{:S(2)}, u32[]{:S(2)}) collective-permute-start(bf16[3008,640]{1,0:T(8,128)(2,1)S(1)} %get-tuple-element.32), channel_id=1, source_target_pairs={{0,8},{8,0},{16,24},{24,16},{32,40},{40,32},{48,56},{56,48},{64,72... | collective-permute-start | bytes 11550728 | tf_op jit(solution)/shard_map/ppermute | solution.py:30
  32.3 22.7 %collective-permute-start.18 = (bf16[704,640]{1,0:T(8,128)(2,1)S(1)}, bf16[704,640]{1,0:T(8,128)(2,1)S(1)}, u32[]{:S(2)}, u32[]{:S(2)}) collective-permute-start(bf16[704,640]{1,0:T(8,128)(2,1)S(1)} %pad_maximum_fusion.refs_1_), channel_id=1, source_target_pairs={{0,32},{8,40},{16,48},{24,56},{32,64},{40,72},{48,80},{56,88},{64,... | collective-permute-start | bytes 2703368 | tf_op jit(solution)/shard_map/ppermute | solution.py:30
  32.3 22.9 %collective-permute-start.21 = (bf16[704,640]{1,0:T(8,128)(2,1)S(1)}, bf16[704,640]{1,0:T(8,128)(2,1)S(1)}, u32[]{:S(2)}, u32[]{:S(2)}) collective-permute-start(bf16[704,640]{1,0:T(8,128)(2,1)S(1)} %pad_maximum_fusion.refs_1_), channel_id=1, source_target_pairs={{0,96},{8,104},{16,112},{24,120},{32,0},{40,8},{48,16},{56,24},{64... | collective-permute-start | bytes 2703368 | tf_op jit(solution)/shard_map/ppermute | solution.py:30
  34.9 20.9 %collective-permute-start.9 = (bf16[704,640]{1,0:T(8,128)(2,1)S(1)}, bf16[704,640]{1,0:T(8,128)(2,1)S(1)}, u32[]{:S(2)}, u32[]{:S(2)}) collective-permute-start(bf16[704,640]{1,0:T(8,128)(2,1)S(1)} %pad_maximum_fusion.refs_1_), channel_id=1, source_target_pairs={{0,16},{8,24},{16,0},{24,8},{32,48},{40,56},{48,32},{56,40},{64,80... | collective-permute-start | bytes 2703368 | tf_op jit(solution)/shard_map/ppermute | solution.py:30
  37.2 25.7 %collective-permute-start.1 = (bf16[288,640]{1,0:T(8,128)(2,1)S(1)}, bf16[288,640]{1,0:T(8,128)(2,1)S(1)}, u32[]{:S(2)}, u32[]{:S(2)}) collective-permute-start(bf16[288,640]{1,0:T(8,128)(2,1)S(1)} %slice.44), channel_id=1, source_target_pairs={{0,32},{8,40},{16,48},{24,56},{32,64},{40,72},{48,80},{56,88},{64,... | collective-permute-start | bytes 1105928 | tf_op jit(solution)/shard_map/ppermute | solution.py:30
  54.9 8.7 %collective-permute-start.5 = (bf16[288,640]{1,0:T(8,128)(2,1)S(1)}, bf16[288,640]{1,0:T(8,128)(2,1)S(1)}, u32[]{:S(2)}, u32[]{:S(2)}) collective-permute-start(bf16[288,640]{1,0:T(8,128)(2,1)S(1)} %slice.45), channel_id=1, source_target_pairs={{0,96},{8,104},{16,112},{24,120},{32,0},{40,8},{48,16},{56,24},{64... | collective-permute-start | bytes 1105928 | tf_op jit(solution)/shard_map/ppermute | solution.py:30
  68.3 25.1 %collective-permute-start.27 = (bf16[2688,640]{1,0:T(8,128)(2,1)S(1)}, bf16[2688,640]{1,0:T(8,128)(2,1)S(1)}, u32[]{:S(2)}, u32[]{:S(2)}) collective-permute-start(bf16[2688,640]{1,0:T(8,128)(2,1)S(1)} %get-tuple-element.37), channel_id=1, source_target_pairs={{0,8},{8,0},{16,24},{24,16},{32,40},{40,32},{48,56},{56,48},{64,72... | collective-permute-start | bytes 10321928 | tf_op jit(solution)/shard_map/ppermute | solution.py:30
  70.8 22.7 %collective-permute-start.10 = (bf16[704,640]{1,0:T(8,128)(2,1)S(1)}, bf16[704,640]{1,0:T(8,128)(2,1)S(1)}, u32[]{:S(2)}, u32[]{:S(2)}) collective-permute-start(bf16[704,640]{1,0:T(8,128)(2,1)S(1)} %collective-permute-done.9.refs_2_), channel_id=1, source_target_pairs={{0,32},{8,40},{16,48},{24,56},{32,64},{40,72},{48,80},{56,88},{64,... | collective-permute-start | bytes 2703368 | tf_op jit(solution)/shard_map/ppermute | solution.py:30
  70.8 22.7 %collective-permute-start.13 = (bf16[704,640]{1,0:T(8,128)(2,1)S(1)}, bf16[704,640]{1,0:T(8,128)(2,1)S(1)}, u32[]{:S(2)}, u32[]{:S(2)}) collective-permute-start(bf16[704,640]{1,0:T(8,128)(2,1)S(1)} %collective-permute-done.9.refs_2_), channel_id=1, source_target_pairs={{0,96},{8,104},{16,112},{24,120},{32,0},{40,8},{48,16},{56,24},{64... | collective-permute-start | bytes 2703368 | tf_op jit(solution)/shard_map/ppermute | solution.py:30
  73.4 17.4 %collective-permute-start.24 = (bf16[576,640]{1,0:T(8,128)(2,1)S(1)}, bf16[576,640]{1,0:T(8,128)(2,1)S(1)}, u32[]{:S(2)}, u32[]{:S(2)}) collective-permute-start(bf16[576,640]{1,0:T(8,128)(2,1)S(1)} %copy-done.6), channel_id=1, source_target_pairs={{0,16},{8,24},{16,0},{24,8},{32,48},{40,56},{48,32},{56,40},{64,80... | collective-permute-start | bytes 2211848 | tf_op jit(solution)/shard_map/ppermute | solution.py:30
  99.0 66.4 %collective-permute-start.28 = (bf16[1984,640]{1,0:T(8,128)(2,1)}, bf16[1984,640]{1,0:T(8,128)(2,1)S(1)}, u32[]{:S(2)}, u32[]{:S(2)}) collective-permute-start(bf16[1984,640]{1,0:T(8,128)(2,1)} %get-tuple-element.42), channel_id=1, source_target_pairs={{0,8},{8,0},{16,24},{24,16},{32,40},{40,32},{48,56},{56,48},{64,72... | collective-permute-start | bytes 7618568 | tf_op jit(solution)/shard_map/ppermute | solution.py:30
  100.1 37.2 %collective-permute-start.16 = (bf16[576,640]{1,0:T(8,128)(2,1)}, bf16[576,640]{1,0:T(8,128)(2,1)}, u32[]{:S(2)}, u32[]{:S(2)}) collective-permute-start(bf16[576,640]{1,0:T(8,128)(2,1)} %copy-done.4), channel_id=1, source_target_pairs={{0,16},{8,24},{16,0},{24,8},{32,48},{40,56},{48,32},{56,40},{64,80... | collective-permute-start | bytes 2211848 | tf_op jit(solution)/shard_map/ppermute | solution.py:30
  102.1 36.0 %collective-permute-start.19 = (bf16[352,640]{1,0:T(8,128)(2,1)}, bf16[352,640]{1,0:T(8,128)(2,1)}, u32[]{:S(2)}, u32[]{:S(2)}) collective-permute-start(bf16[352,640]{1,0:T(8,128)(2,1)} %slice.48), channel_id=1, source_target_pairs={{0,32},{8,40},{16,48},{24,56},{32,64},{40,72},{48,80},{56,88},{64,... | collective-permute-start | bytes 1351688 | tf_op jit(solution)/shard_map/ppermute | solution.py:30
  104.7 13.6 %collective-permute-start.30 = (bf16[2,128]{1,0:T(2,128)(2,1)S(1)}, bf16[2,128]{1,0:T(2,128)(2,1)S(1)}, u32[]{:S(2)}, u32[]{:S(2)}) collective-permute-start(bf16[2,128]{1,0:T(2,128)(2,1)S(1)} %pad_maximum_fusion.3), channel_id=1, source_target_pairs={{0,16},{8,24},{16,0},{24,8},{32,48},{40,56},{48,32},{56,40},{64,80... | collective-permute-start | bytes 1544 | tf_op jit(solution)/shard_map/ppermute | solution.py:30
  118.4 5.1 %collective-permute-start.32 = (bf16[4,128]{1,0:T(4,128)(2,1)S(1)}, bf16[4,128]{1,0:T(4,128)(2,1)S(1)}, u32[]{:S(2)}, u32[]{:S(2)}) collective-permute-start(bf16[4,128]{1,0:T(4,128)(2,1)S(1)} %pad_maximum_fusion.2), channel_id=1, source_target_pairs={{0,64},{8,72},{16,80},{24,88},{32,96},{40,104},{48,112},{56,120},{... | collective-permute-start | bytes 3080 | tf_op jit(solution)/shard_map/ppermute | solution.py:30
  125.0 4.0 %collective-permute-start.34 = (bf16[16,128]{1,0:T(8,128)(2,1)S(1)}, bf16[16,128]{1,0:T(8,128)(2,1)S(1)}, u32[]{:S(2)}, u32[]{:S(2)}) collective-permute-start(bf16[16,128]{1,0:T(8,128)(2,1)S(1)} %concatenate.33), channel_id=1, source_target_pairs={{0,2},{1,3},{2,4},{3,5},{4,6},{5,7},{6,0},{7,1},{8,10},{9,11},{10,... | collective-permute-start | bytes 12296 | tf_op jit(solution)/shard_map/ppermute | solution.py:30
  131.8 4.8 %collective-permute-start.37 = (bf16[64,128]{1,0:T(8,128)(2,1)S(1)}, bf16[64,128]{1,0:T(8,128)(2,1)S(1)}, u32[]{:S(2)}, u32[]{:S(2)}) collective-permute-start(bf16[64,128]{1,0:T(8,128)(2,1)S(1)} %concatenate.34), channel_id=1, source_target_pairs={{0,1},{1,0},{2,3},{3,2},{4,5},{5,4},{6,7},{7,6},{8,9},{9,8},{10,11... | collective-permute-start | bytes 49160 | tf_op jit(solution)/shard_map/ppermute | solution.py:30
  134.7 15.3 %collective-permute-start.22 = (bf16[352,640]{1,0:T(8,128)(2,1)S(1)}, bf16[352,640]{1,0:T(8,128)(2,1)S(1)}, u32[]{:S(2)}, u32[]{:S(2)}) collective-permute-start(bf16[352,640]{1,0:T(8,128)(2,1)S(1)} %slice.49), channel_id=1, source_target_pairs={{0,96},{8,104},{16,112},{24,120},{32,0},{40,8},{48,16},{56,24},{64... | collective-permute-start | bytes 1351688 | tf_op jit(solution)/shard_map/ppermute | solution.py:30
  136.7 10.0 %collective-permute-start.2 = (bf16[288,640]{1,0:T(8,128)(2,1)}, bf16[288,640]{1,0:T(8,128)(2,1)}, u32[]{:S(2)}, u32[]{:S(2)}) collective-permute-start(bf16[288,640]{1,0:T(8,128)(2,1)} %copy-done.13), channel_id=1, source_target_pairs={{0,16},{8,24},{16,0},{24,8},{32,48},{40,56},{48,32},{56,40},{64,80... | collective-permute-start | bytes 1105928 | tf_op jit(solution)/shard_map/ppermute | solution.py:30
  137.2 12.3 %collective-permute-start.6 = (bf16[288,640]{1,0:T(8,128)(2,1)}, bf16[288,640]{1,0:T(8,128)(2,1)}, u32[]{:S(2)}, u32[]{:S(2)}) collective-permute-start(bf16[288,640]{1,0:T(8,128)(2,1)} %copy-done.14), channel_id=1, source_target_pairs={{0,16},{8,24},{16,0},{24,8},{32,48},{40,56},{48,32},{56,40},{64,80... | collective-permute-start | bytes 1105928 | tf_op jit(solution)/shard_map/ppermute | solution.py:30
  138.2 20.2 %collective-permute-start.20 = (bf16[352,640]{1,0:T(8,128)(2,1)}, bf16[352,640]{1,0:T(8,128)(2,1)S(1)}, u32[]{:S(2)}, u32[]{:S(2)}) collective-permute-start(bf16[352,640]{1,0:T(8,128)(2,1)} %collective-permute-done.19.refs_1_), channel_id=1, source_target_pairs={{0,8},{8,0},{16,24},{24,16},{32,40},{40,32},{48,56},{56,48},{64,72... | collective-permute-start | bytes 1351688 | tf_op jit(solution)/shard_map/ppermute | solution.py:30
  146.7 12.5 %collective-permute-start.11 = (bf16[352,640]{1,0:T(8,128)(2,1)S(1)}, bf16[352,640]{1,0:T(8,128)(2,1)}, u32[]{:S(2)}, u32[]{:S(2)}) collective-permute-start(bf16[352,640]{1,0:T(8,128)(2,1)S(1)} %slice.46), channel_id=1, source_target_pairs={{0,32},{8,40},{16,48},{24,56},{32,64},{40,72},{48,80},{56,88},{64,... | collective-permute-start | bytes 1351688 | tf_op jit(solution)/shard_map/ppermute | solution.py:30
  149.6 12.3 %collective-permute-start.14 = (bf16[352,640]{1,0:T(8,128)(2,1)S(1)}, bf16[352,640]{1,0:T(8,128)(2,1)}, u32[]{:S(2)}, u32[]{:S(2)}) collective-permute-start(bf16[352,640]{1,0:T(8,128)(2,1)S(1)} %slice.47), channel_id=1, source_target_pairs={{0,96},{8,104},{16,112},{24,120},{32,0},{40,8},{48,16},{56,24},{64... | collective-permute-start | bytes 1351688 | tf_op jit(solution)/shard_map/ppermute | solution.py:30
  150.0 14.6 %collective-permute-start.23 = (bf16[352,640]{1,0:T(8,128)(2,1)S(1)}, bf16[352,640]{1,0:T(8,128)(2,1)S(1)}, u32[]{:S(2)}, u32[]{:S(2)}) collective-permute-start(bf16[352,640]{1,0:T(8,128)(2,1)S(1)} %collective-permute-done.22.refs_2_), channel_id=1, source_target_pairs={{0,8},{8,0},{16,24},{24,16},{32,40},{40,32},{48,56},{56,48},{64,72... | collective-permute-start | bytes 1351688 | tf_op jit(solution)/shard_map/ppermute | solution.py:30
  159.2 11.4 %collective-permute-start.17 = (bf16[576,640]{1,0:T(8,128)(2,1)}, bf16[576,640]{1,0:T(8,128)(2,1)S(1)}, u32[]{:S(2)}, u32[]{:S(2)}) collective-permute-start(bf16[576,640]{1,0:T(8,128)(2,1)} %collective-permute-done.16.refs_0_), channel_id=1, source_target_pairs={{0,8},{8,0},{16,24},{24,16},{32,40},{40,32},{48,56},{56,48},{64,72... | collective-permute-start | bytes 2211848 | tf_op jit(solution)/shard_map/ppermute | solution.py:30
  159.2 15.0 %collective-permute-start.12 = (bf16[352,640]{1,0:T(8,128)(2,1)}, bf16[352,640]{1,0:T(8,128)(2,1)}, u32[]{:S(2)}, u32[]{:S(2)}) collective-permute-start(bf16[352,640]{1,0:T(8,128)(2,1)} %collective-permute-done.11.refs_2_), channel_id=1, source_target_pairs={{0,8},{8,0},{16,24},{24,16},{32,40},{40,32},{48,56},{56,48},{64,72... | collective-permute-start | bytes 1351688 | tf_op jit(solution)/shard_map/ppermute | solution.py:30
  161.8 12.3 %collective-permute-start.15 = (bf16[352,640]{1,0:T(8,128)(2,1)}, bf16[352,640]{1,0:T(8,128)(2,1)}, u32[]{:S(2)}, u32[]{:S(2)}) collective-permute-start(bf16[352,640]{1,0:T(8,128)(2,1)} %collective-permute-done.14.refs_3_), channel_id=1, source_target_pairs={{0,8},{8,0},{16,24},{24,16},{32,40},{40,32},{48,56},{56,48},{64,72... | collective-permute-start | bytes 1351688 | tf_op jit(solution)/shard_map/ppermute | solution.py:30
  165.4 8.7 %collective-permute-start.3 = (bf16[288,640]{1,0:T(8,128)(2,1)}, bf16[288,640]{1,0:T(8,128)(2,1)}, u32[]{:S(2)}, u32[]{:S(2)}) collective-permute-start(bf16[288,640]{1,0:T(8,128)(2,1)} %collective-permute-done.2.refs_0_), channel_id=1, source_target_pairs={{0,8},{8,0},{16,24},{24,16},{32,40},{40,32},{48,56},{56,48},{64,72... | collective-permute-start | bytes 1105928 | tf_op jit(solution)/shard_map/ppermute | solution.py:30
  165.4 8.7 %collective-permute-start.7 = (bf16[288,640]{1,0:T(8,128)(2,1)}, bf16[288,640]{1,0:T(8,128)(2,1)}, u32[]{:S(2)}, u32[]{:S(2)}) collective-permute-start(bf16[288,640]{1,0:T(8,128)(2,1)} %collective-permute-done.6.refs_1_), channel_id=1, source_target_pairs={{0,8},{8,0},{16,24},{24,16},{32,40},{40,32},{48,56},{56,48},{64,72... | collective-permute-start | bytes 1105928 | tf_op jit(solution)/shard_map/ppermute | solution.py:30
  (28 other events, 225.3 us)
